TPU v7x, 128 devices: a whole 4x4x4 slice. The times are simulated.
128 devices in a mesh: seq: 32 (over z, y, core), chan: 4 (over x).
Axes of the slice: x: 4, y: 4, z: 4, core: 2. Of those that a mesh axis runs over, the one named last changes fastest.
Arguments:
- features: bfloat16 [393216, 1024], P('seq', 'chan'), may hold values from -6 to 6
- gate_input: bfloat16 [393216, 1024], P('seq', 'chan'), may hold values from -6 to 6
- input_map: bfloat16 [393216, 128], P('seq', 'chan'), may hold values from -6 to 6
- output_map: bfloat16 [393216, 128], P('seq', 'chan'), may hold values from -6 to 6
- step_raw: float32 [393216, 16], P('seq', 'chan'), may hold values from -4 to 4
- step_bias: float32 [16], P('chan')
- decay_log: float32 [16], P('chan')
- skip_gain: float32 [16], P('chan'), may hold values from 0.5 to 1.5
- norm_gain: float32 [1024], P('chan'), may hold values from 0.1 to 1.9
- tissue: int32 [768, 2], P('seq'), may hold values from 0 to 512, as said below
Outputs:
- mixed: bfloat16 [393216, 1024], P('seq', 'chan')
Inputs may be any that keep to these rules, and one draw needn't show every extreme that they name: tissue[r, 0] <= tissue[r, 1]; a row with equal values holds no tissue.
All inputs are finite; a program needn't handle non-finite values.
Results may differ from a plain program's by a relative error of at most 0.0039.
Values may be sent and summed in bfloat16 or wider, within the bound.
A program may use at most 192 MiB of HBM per device.

v0:
```python
import jax
import jax.numpy as jnp
from jax import lax
from jax.sharding import Mesh
from jax.sharding import PartitionSpec as P

D = 1024
ROW = 512
SEQ = ("seq_0", "seq_1", "seq_2")


EPS = 1e-05


def gather_turned(arrays, axis, dims):
    turned = [jnp.moveaxis(a, dim, 0) for a, dim in zip(arrays, dims)]
    widths = [t[0].size for t in turned]
    both = jnp.concatenate([t.reshape(-1, w) for t, w in zip(turned, widths)], axis=1)
    filled = lax.all_gather(both, axis, axis=0, tiled=True)
    tiles = jnp.split(filled, [sum(widths[:k]) for k in range(1, len(widths))], axis=1)
    return tuple(
        (
            jnp.moveaxis(b.reshape(-1, *t.shape[1:]), 0, dim)
            for b, t, dim in zip(tiles, turned, dims)
        )
    )


def nothing_yet(array, identity):
    return jax.tree.map(
        lambda a, e: jnp.broadcast_to(jnp.asarray(e, a.dtype), a.shape), array, identity
    )


def entering(array, axes, combine, identity):
    before = start = nothing_yet(array, identity)
    so_far = array
    for axis in reversed(axes):
        peers, mine = (lax.axis_size(axis), lax.axis_index(axis))
        pieces = jax.tree.map(lambda part: lax.all_gather(part, axis), so_far)
        inside, so_far = (start, start)
        for k in range(peers):
            passed = k < mine
            so_far = combine(so_far, jax.tree.map(lambda part: part[k], pieces))
            inside = jax.tree.map(lambda new, old: jnp.where(passed, new, old), so_far, inside)
        before = combine(inside, before)
    return before


def copy_for_each(array, axis):
    copies = jnp.broadcast_to(array, (lax.axis_size(axis), *array.shape))
    return lax.all_to_all(copies, axis, split_axis=0, concat_axis=0, tiled=True)


def over_copies(array, axis):
    everything = copy_for_each(array, axis)
    return jnp.sum(everything, axis=0)


def group_state(state_in, x_row, b_row, running, step_row):
    row_total = running[-1]
    scaled = jnp.exp(row_total[None, :] - running) * step_row
    b_scaled = (scaled.T[:, :, None] * b_row.astype(jnp.float32)[None]).astype(jnp.bfloat16)
    fresh = jnp.einsum("hsn,shp->hnp", b_scaled, x_row, preferred_element_type=jnp.float32)
    return jnp.exp(row_total)[:, None, None] * state_in + fresh


def row_block(state_in, x_row, b_row, c_row, log_row, step_row):
    running = jnp.cumsum(log_row, axis=0)
    length = log_row.shape[0]
    order = jnp.arange(length, dtype=jnp.int32)
    causal = (order[:, None] >= order[None, :])[None]
    scores = jnp.dot(c_row, b_row.T, preferred_element_type=jnp.float32)
    per_head = running.T
    gap_log = per_head[:, :, None] - per_head[:, None, :]
    damping = jnp.where(causal, jnp.exp(jnp.where(causal, gap_log, 0.0)), 0.0)
    weights = (scores[None] * damping * step_row.T[:, None, :]).astype(jnp.bfloat16)
    inner = jnp.einsum("hts,shp->thp", weights, x_row, preferred_element_type=jnp.float32)
    carried = jnp.exp(running)[:, :, None] * jnp.einsum(
        "tn,hnp->thp", c_row.astype(jnp.float32), state_in, precision=lax.Precision.HIGH
    )
    state_out = group_state(state_in, x_row, b_row, running, step_row)
    return (state_out, inner + carried, running)


def combine(earlier, later):
    return (earlier[0] + later[0], jnp.exp(later[0])[:, None, None] * earlier[1] + later[1])


def per_device(
    features,
    gate_input,
    input_map,
    output_map,
    step_raw,
    step_bias,
    decay_log,
    skip_gain,
    norm_gain,
    tissue,
):
    b_full, c_full = gather_turned((input_map, output_map), "chan", (1, 1))
    tokens_here = features.shape[0]
    head_count = step_bias.shape[0]
    head_width = features.shape[1] // head_count
    state_width = b_full.shape[1]
    row_count = tokens_here // ROW
    position = jnp.arange(ROW, dtype=jnp.int32)
    inside = ((position[None, :] >= tissue[:, 0:1]) & (position[None, :] < tissue[:, 1:2])).astype(
        jnp.float32
    )
    step_size = (
        jax.nn.softplus(step_raw.reshape(row_count, ROW, head_count) + step_bias)
        * inside[:, :, None]
    )
    log_decay = -jnp.exp(decay_log) * step_size
    x_rows = features.reshape(row_count, ROW, head_count, head_width)
    b_rows = b_full.reshape(row_count, ROW, state_width)
    c_rows = c_full.reshape(row_count, ROW, state_width)
    zero_state = jnp.zeros((head_count, state_width, head_width), jnp.float32)
    zero_log = jnp.zeros((head_count,), jnp.float32)

    def local_row(carry, items):
        log_total, state_in = carry
        x_row, b_row, c_row, log_row, step_row = items
        state_out, y_row, running = row_block(state_in, x_row, b_row, c_row, log_row, step_row)
        return ((log_total + running[-1], state_out), (y_row, log_total[None, :] + running))

    (log_total, state_end), (y_rows, band_running) = lax.scan(
        local_row, (zero_log, zero_state), (x_rows, b_rows, c_rows, log_decay, step_size)
    )
    incoming = entering((log_total, state_end), SEQ, combine, (zero_log, zero_state))
    correction = jnp.einsum(
        "rtn,hnp->rthp", c_rows.astype(jnp.float32), incoming[1], precision=lax.Precision.HIGH
    )
    y_rows = y_rows + jnp.exp(band_running)[..., None] * correction
    y_rows = y_rows + skip_gain[:, None] * x_rows.astype(jnp.float32)
    gated = y_rows.reshape(tokens_here, features.shape[1]) * jax.nn.silu(
        gate_input.astype(jnp.float32)
    )
    square_sum = over_copies(jnp.sum(gated * gated, axis=-1), "chan")
    scale = lax.rsqrt(square_sum / D + EPS)
    return (gated * scale[:, None] * norm_gain).astype(jnp.bfloat16)


def solution(mesh):
    split = Mesh(
        mesh.devices.reshape(4, 4, 2, mesh.shape["chan"]), ("seq_0", "seq_1", "seq_2", "chan")
    )
    placed = (
        P(SEQ, "chan"),
        P(SEQ, "chan"),
        P(SEQ, "chan"),
        P(SEQ, "chan"),
        P(SEQ, "chan"),
        P("chan"),
        P("chan"),
        P("chan"),
        P("chan"),
        P(SEQ, None),
    )
    return jax.shard_map(
        per_device, mesh=split, in_specs=placed, out_specs=P(SEQ, "chan"), check_vma=False
    )
```

profile of v0, /device:TPU:0, one launch (start us, length us, event | category | flops | bytes accessed | tf_op | source)
XLA Modules:
  0.0 499.6 jit_solution(18182950658834751226)
XLA Ops:
  9.3 18.8 %reshape.353 = bf16[24,512,4,64]{3,2,1,0:T(4,128)(2,1)} reshape(bf16[12288,256]{1,0:T(8,128)(2,1)} %param.12) | data formatting | bytes 12582912 | tf_op jit(solution)/shard_map/reshape | solution.py:117
  28.1 18.5 %copy.93 = bf16[24,512,4,64]{1,3,2,0:T(8,128)(2,1)} copy(bf16[24,512,4,64]{3,2,1,0:T(4,128)(2,1)} %reshape.353) | data formatting | bytes 12582912
  49.2 8.7 %copy.96 = bf16[12288,256]{0,1:T(8,128)(2,1)} copy(bf16[12288,256]{1,0:T(8,128)(2,1)} %param.13) | data formatting | bytes 12582912 | tf_op args[1]
  59.1 18.3 %all-gather.6.cloned.1.call-done = bf16[128,24576]{1,0:T(8,128)(2,1)} async-done(((bf16[32,24576]{1,0:T(8,128)(2,1)}), bf16[128,24576]{1,0:T(8,128)(2,1)}) %all-gather.6.cloned.1.call-update) | async-done | bytes 6291472 | tf_op jit(solution)/shard_map/all_gather | solution.py:19
  77.4 5.0 %slice_bitcast_fusion = (bf16[12288,128]{0,1:T(8,128)(2,1)}, bf16[12288,128]{0,1:T(8,128)(2,1)S(1)}) fusion(bf16[128,24576]{1,0:T(8,128)(2,1)} %all-gather.6.cloned.1.call-done), kind=kLoop, calls=%fused_computation.52 | loop fusion | bytes 12582912 | tf_op jit(solution)/shard_map/transpose | solution.py:23
  88.8 259.3 %while.18 = (s32[]{:T(128)}, f32[4]{0:T(128)S(1)}, f32[4,128,64]{1,2,0:T(8,128)S(1)}, f32[24,512,4,64]{1,3,2,0:T(8,128)}, f32[24,512,4]{1,2,0:T(4,128)}, /*index...) while((s32[]{:T(128)}, f32[4]{0:T(128)S(1)}, ...), condition=%wide.region_3.4_spmd.clone.clone, body=%wide.region_0.3_spmd.clone.sunk.clone | while | flops 343316544 | bytes 6613640 | solution.py:129
  95.4 3.5 fusion.118
  117.0 3.5 fusion.118
  138.6 3.5 fusion.118
  149.5 3.5 fusion.118
  171.1 3.5 fusion.118
  181.9 3.5 fusion.118
  203.5 3.5 fusion.118
  225.1 3.5 fusion.118
  235.9 3.5 fusion.118
  257.5 3.5 fusion.118
  268.3 3.5 fusion.118
  279.2 3.5 fusion.118
  290.0 3.5 fusion.118
  311.5 3.5 fusion.118
  343.9 3.5 fusion.118
  355.2 13.9 %all_gather.38 = f32[4,4,128,64]{2,3,1,0:T(8,128)} all-gather(f32[1,4,128,64]{2,3,1,0:T(8,128)S(1)} %fusion.37), channel_id=1, replica_groups=mesh['seq_0'=4,'seq_1'=4,'seq_2'=2,'chan'=4] {'seq_1'}, dimensions={0}, use_global_device_ids=true | all-gather | bytes 655360 | tf_op jit(solution)/shard_map/all_gather | solution.py:40
  369.1 10.6 %all-reduce.1 = f32[16]{0:T(128)S(1)} all-reduce(f32[16]{0:T(128)} %copy-done.6), channel_id=4, replica_groups=mesh['seq_0'=4,'seq_1'=4,'seq_2'=2,'chan'=4] {'seq_1'}, use_global_device_ids=true, to_apply=%add.1 | all-reduce | flops 16 | bytes 128
  381.1 13.3 %all_gather.39 = f32[4,4,128,64]{2,3,1,0:T(8,128)S(1)} all-gather(f32[1,4,128,64]{2,3,1,0:T(8,128)S(1)} %slice_add_fusion.4), channel_id=1, replica_groups=mesh['seq_0'=4,'seq_1'=4,'seq_2'=2,'chan'=4] {'seq_0'}, dimensions={0}, use_global_device_ids=true | all-gather | bytes 655360 | tf_op jit(solution)/shard_map/all_gather | solution.py:40
  394.3 9.4 %all-gather.3 = f32[4,1,4]{2,1,0:T(1,128)S(1)} all-gather(f32[1,1,4]{2,1,0:T(1,128)S(1)} %get-tuple-element.209), channel_id=1, replica_groups=mesh['seq_0'=4,'seq_1'=4,'seq_2'=2,'chan'=4] {'seq_0'}, dimensions={0}, use_global_device_ids=true | all-gather | bytes 80 | tf_op jit(solution)/shard_map/all_gather | solution.py:40
  403.8 13.8 %multiply_add_fusion = f32[24,512,4,64]{1,3,2,0:T(8,128)} fusion(bf16[24,512,4,64]{1,3,2,0:T(8,128)(2,1)} %get-tuple-element.356, f32[24,512,4,64]{1,3,2,0:T(8,128)} %get-tuple-element.60, f32[4]{0:T(128)S(1)} %copy-done.4, f32[24,512,4]{1,2,0:T(4,128)} %exp.140, bf16[24,512,128,1]{2,1,3,0:T(8,128)(2,1)S(1)} %bitcast.190, ...), kind=kOutput, calls=%fused_computation.51 | convolution fusion | flops 2432532480 | bytes 36115976 | tf_op jit(solution)/shard_map/rtn,hnp->rthp/dot_general | solution.py:133
  417.6 16.6 %copy.95 = f32[24,512,4,64]{1,0,3,2:T(8,128)} copy(f32[24,512,4,64]{1,3,2,0:T(8,128)} %multiply_add_fusion) | data formatting | bytes 25165824 | tf_op jit(solution)/shard_map/add | solution.py:137
  434.1 20.8 %copy.104 = f32[32,8,24,512]{3,1,2,0:T(8,128)} copy(f32[32,8,24,512]{3,2,1,0:T(8,128)} %bitcast.187) | data formatting | bytes 25165824
  455.0 7.2 %multiply_reduce_fusion = f32[12288]{0:T(1024)S(1)} fusion(f32[12288,256]{0,1:T(8,128)} %bitcast.183, bf16[12288,256]{0,1:T(8,128)(2,1)S(1)} %bitcast.186), kind=kLoop, calls=%fused_computation.50 | loop fusion | flops 25153536 | bytes 18923520 | tf_op jit(solution)/shard_map/reduce_sum | solution.py:141
  462.3 9.8 %all_to_all.6 = f32[4,1,12288]{2,1,0:T(1,128)S(1)} all-to-all(f32[4,1,12288]{2,1,0:T(1,128)S(1)} %broadcast_in_dim.52), channel_id=1, replica_groups=mesh['seq_0'=4,'seq_1'=4,'seq_2'=2,'chan'=4] {'chan'}, dimensions={0} | all-to-all | bytes 393216 | tf_op jit(solution)/shard_map/all_to_all | solution.py:52
  472.3 11.8 %multiply_convert_fusion.12 = bf16[12288,256]{0,1:T(8,128)(2,1)} fusion(f32[256]{0:T(256)S(1)} %copy-done.1, f32[12288]{0:T(1024)S(1)} %add_rsqrt_fusion, f32[12288,256]{0,1:T(8,128)} %bitcast.184, bf16[12288,256]{0,1:T(8,128)(2,1)} %copy.96), kind=kLoop, calls=%fused_computation.49 | loop fusion | flops 28311552 | bytes 25216000 | tf_op jit(solution)/shard_map/convert_element_type | solution.py:143
  484.2 8.6 %copy.98 = bf16[12288,256]{1,0:T(8,128)(2,1)} copy(bf16[12288,256]{0,1:T(8,128)(2,1)} %multiply_convert_fusion.12) | data formatting | bytes 12582912 | tf_op jit(solution)/shard_map/convert_element_type | solution.py:143
  (471 shorter events, 225.6 us)
Async XLA Ops:
  6.5 70.9 %all-gather.6.cloned.1.call-start = ((), (), s32[]{:S(2)}) async-start(), calls=%async_computation.1 | async-start | bytes 7864320 | tf_op jit(solution)/shard_map/all_gather | solution.py:19
  28.1 18.5 %copy-start.8 = (u32[128]{0:T(128)S(1)}, u32[128]{0:T(128)}, u32[]{:S(2)}) copy-start(u32[128]{0:T(128)} %constant.68) | copy-start | bytes 1540
  28.1 19.2 %copy-start.7 = (u32[128]{0:T(128)S(1)}, u32[128]{0:T(128)}, u32[]{:S(2)}) copy-start(u32[128]{0:T(128)} %constant.63) | copy-start | bytes 1540
  49.2 8.8 %copy-start.5 = (f32[4]{0:T(128)S(1)}, f32[4]{0:T(128)}, u32[]{:S(2)}) copy-start(f32[4]{0:T(128)} %param.18) | copy-start | bytes 52
  49.2 8.8 %copy-start.2 = (s32[24,2]{0,1:T(2,128)S(1)}, s32[24,2]{0,1:T(2,128)}, u32[]{:S(2)}) copy-start(s32[24,2]{0,1:T(2,128)} %param.21) | copy-start | bytes 580
  49.2 8.9 %copy-start = (f32[12288,4]{0,1:T(4,128)S(1)}, f32[12288,4]{0,1:T(4,128)}, u32[]{:S(2)}) copy-start(f32[12288,4]{0,1:T(4,128)} %param.16) | copy-start | bytes 589828
  49.2 8.9 %copy-start.3 = (f32[4]{0:T(128)S(1)}, f32[4]{0:T(128)}, u32[]{:S(2)}) copy-start(f32[4]{0:T(128)} %param.17) | copy-start | bytes 52
  88.8 315.0 %copy-start.4 = (f32[4]{0:T(128)S(1)}, f32[4]{0:T(128)}, u32[]{:S(2)}) copy-start(f32[4]{0:T(128)} %param.19) | copy-start | bytes 52
  354.5 0.6 copy-start.6
  417.6 37.4 %slice-start = ((s8[6291456]{0:T(1024)(128)(4,1)}), s8[4194304]{0:T(1024)(128)(4,1)S(1)}, s32[]{:S(2)}) async-start(s8[6291456]{0:T(1024)(128)(4,1)} %bitcast.185), calls=%async_computation.2 | async-start | bytes 8388608
  434.1 20.8 %slice-start.1 = ((s8[6291456]{0:T(1024)(128)(4,1)}), s8[2097152]{0:T(1024)(128)(4,1)S(1)}, s32[]{:S(2)}) async-start(s8[6291456]{0:T(1024)(128)(4,1)} %bitcast.185), calls=%async_computation.3 | async-start | bytes 4194304
  455.0 17.3 %copy-start.1 = (f32[256]{0:T(256)S(1)}, f32[256]{0:T(256)}, u32[]{:S(2)}) copy-start(f32[256]{0:T(256)} %param.20) | copy-start | bytes 3076
Sparse Core Ops, SparseCore 0:
  9.3 68.0 all-gather.5
where the time goes:
time: 505 us; the launch traced here: 500 us
  matrix products  169 us (33%)
  local copies, waits for them, and re-layouts  133 us (26%)
  other arithmetic  102 us (20%)
  blocking collectives  61.4 us (12%)
  waiting for transfers between devices  18.4 us (4%)
  between operations  14.9 us (3%)
    dot_general x24, matrix products, row_block(): jnp.einsum('hts,shp->thp', weights, x_row, preferred_element_type=jnp.flo...  84.1 us
    unnamed x30, local copies, waits for them, and re-layouts  50.2 us
    all_gather x4, blocking collectives, entering(): pieces = jax.tree.map(lambda part: lax.all_gather(part, axis), so_far)  38.5 us
    dot_general x24, matrix products, group_state(): jnp.einsum('hsn,shp->hnp', b_scaled, x_row, preferred_element_type=jnp.fl...  34.4 us
    another operation x48, other arithmetic  33.4 us
    dot_general x24, matrix products, row_block(): scores = jnp.dot(c_row, b_row.T, preferred_element_type=jnp.float32)  28.9 us
    mul x24, other arithmetic, group_state(): scaled.T[:, :, None] * b_row.astype(jnp.float32)[None]  22.3 us
    reshape x1, local copies, waits for them, and re-layouts, per_device(): x_rows = features.reshape(row_count, ROW, head_count, head_width)  18.8 us
  transfers between devices with their start and end apart: 1, of which 1 were waited for; matrix products, arithmetic and copies ran while one was open for 10% of the time, Pallas kernels for 0%

commit v1 on v0

v1 whole, which is shorter than its diff:
```python
import functools

import jax
import jax.numpy as jnp
from jax import lax
from jax.experimental import pallas as pl
from jax.experimental.pallas import tpu as pltpu
from jax.sharding import Mesh
from jax.sharding import PartitionSpec as P

D = 1024
ROW = 512
EPS = 1e-05
SEQ = ("seq_0", "seq_1", "seq_2")
Q = 128
H = 4
W = 64
N = 128
LOG2E = 1.4426950408889634
F32 = jnp.float32
BF16 = jnp.bfloat16


def softplus(x):
    u = jnp.exp(-jnp.abs(x))
    series = u * (1.0 + u * (-1 / 2 + u * (1 / 3 + u * (-1 / 4 + u * (1 / 5 + u * (-1 / 6 + u * (1 / 7)))))))
    return jnp.maximum(x, 0.0) + jnp.where(u < 0.0625, series, jnp.log(1.0 + u))


def exact_dot(a, b):
    hi = a.astype(BF16)
    rest = a - hi.astype(F32)
    mid = rest.astype(BF16)
    low = (rest - mid.astype(F32)).astype(BF16)
    dot = lambda p: jnp.dot(p, b, preferred_element_type=F32)
    return dot(hi) + (dot(mid) + dot(low))


def decay_group(g, group, raw_ref, bias_ref, rate_ref, tissue_ref, tri, cols_ref, rows_ref, sums_ref, total):
    lane = lax.broadcasted_iota(jnp.int32, (H, Q), 1)
    steps = []
    for k in range(group):
        c = g * group + k
        r = c // (ROW // Q)
        raw = raw_ref[:, pl.ds(pl.multiple_of(c * Q, Q), Q)]
        place = lane + (c % (ROW // Q)) * Q
        inside = (place >= tissue_ref[2 * r]) & (place < tissue_ref[2 * r + 1])
        steps.append(jnp.where(inside, softplus(raw + bias_ref[...]), 0.0))
    step = jnp.concatenate(steps, axis=0)
    log2_decay = step * jnp.concatenate([rate_ref[...]] * group, axis=0)
    both = exact_dot(log2_decay, tri)
    run, tot = both[:, :Q], both[:, Q:]
    key = run - jnp.log(step) * LOG2E
    left = jnp.exp2(tot - run) * step
    grown = jnp.exp2(run)
    for k in range(group):
        c = g * group + k
        at = slice(k * H, (k + 1) * H)
        cols_ref[c] = jnp.concatenate([run[at], grown[at]], axis=0)
        rows_ref[c] = jnp.concatenate([key[at], left[at]], axis=0)
        sums_ref[c] = jnp.concatenate([tot[at], total], axis=0)
        total = total + tot[at]
    return total


def triangle():
    i = lax.broadcasted_iota(jnp.int32, (Q, 2 * Q), 0)
    j = lax.broadcasted_iota(jnp.int32, (Q, 2 * Q), 1)
    return jnp.where((i <= j), 1.0, 0.0).astype(BF16)


def per_head_lanes(rows, k):
    lane = lax.broadcasted_iota(jnp.int32, (1, 2 * W), 1)
    pieces = [
        jnp.where(lane < W, rows[k + 2 * p : k + 2 * p + 1], rows[k + 2 * p + 1 : k + 2 * p + 2])
        for p in range(H // 2)
    ]
    return jnp.concatenate(pieces, axis=1)


def split_pair(x, p):
    lane = lax.broadcasted_iota(jnp.int32, (Q, 2 * W), 1)
    pair = x[:, 2 * W * p : 2 * W * (p + 1)]
    zero = jnp.zeros_like(pair)
    return jnp.concatenate([jnp.where(lane < W, pair, zero), jnp.where(lane < W, zero, pair)], axis=0)


def fresh_state(bt, left, pairs):
    b = bt.astype(F32)
    out = []
    for p in range(H // 2):
        scaled = [(b * left[h : h + 1]).astype(BF16) for h in (2 * p, 2 * p + 1)]
        out.append(jnp.dot(jnp.concatenate(scaled, axis=1), pairs[p], preferred_element_type=F32))
    return jnp.concatenate(out, axis=1)


def band_state_chunk(x, bt, rows, sums, total):
    ahead = total - sums[H : 2 * H] - sums[0:H]
    left = rows[H : 2 * H] * jnp.exp2(ahead)
    return fresh_state(bt, left, [split_pair(x, p) for p in range(H // 2)])


def output_chunk(x, gate, bt, ct, cols, rows, sums, skip, state):
    c = ct.T
    pairs = [split_pair(x, p) for p in range(H // 2)]
    scores = jnp.dot(c, bt, preferred_element_type=F32)
    t = lax.broadcasted_iota(jnp.int32, (Q, Q), 0)
    s = lax.broadcasted_iota(jnp.int32, (Q, Q), 1)
    scores = jnp.where(t >= s, scores, 0.0)
    carried = jnp.dot(c, state.astype(BF16), preferred_element_type=F32)
    col = cols.T
    lane = lax.broadcasted_iota(jnp.int32, (Q, 2 * W), 1)
    inner = []
    grown = []
    for p in range(H // 2):
        weights = []
        for h in (2 * p, 2 * p + 1):
            gap = jnp.minimum(col[:, h : h + 1] - rows[h : h + 1], 127.0)
            weights.append((scores * jnp.exp2(gap)).astype(BF16))
        inner.append(jnp.dot(jnp.concatenate(weights, axis=1), pairs[p], preferred_element_type=F32))
        k = H + 2 * p
        grown.append(jnp.where(lane < W, col[:, k : k + 1], col[:, k + 1 : k + 2]))
    inner = jnp.concatenate(inner, axis=1)
    grown = jnp.concatenate(grown, axis=1)
    y = inner + grown * carried + skip * x.astype(F32)
    half = gate.astype(F32) * 0.5
    gated = y * (half + half * jnp.tanh(half))
    square = gated * gated
    square = square[:, :Q] + square[:, Q:]
    squares = jnp.sum(square.T, axis=0, keepdims=True)
    state = jnp.exp2(per_head_lanes(sums, 0)) * state + fresh_state(bt, rows[H : 2 * H], pairs)
    return gated, squares, state


def decay_kernel(group, raw_ref, bias_ref, rate_ref, tissue_ref, cols_ref, rows_ref, sums_ref, total_ref):
    tri = triangle()
    count = cols_ref.shape[0] // group
    step = lambda g, total: decay_group(
        g, group, raw_ref, bias_ref, rate_ref, tissue_ref, tri, cols_ref, rows_ref, sums_ref, total
    )
    total_ref[...] = lax.fori_loop(0, count, step, jnp.zeros((H, Q), F32))


def state_kernel(x_ref, bt_ref, rows_ref, sums_ref, total_ref, state_ref):
    @pl.when(pl.program_id(0) == 0)
    def _():
        state_ref[...] = jnp.zeros_like(state_ref)

    acc = state_ref[...]
    for k in range(ROW // Q):
        acc = acc + band_state_chunk(
            x_ref[k * Q : (k + 1) * Q, :],
            bt_ref[:, k * Q : (k + 1) * Q],
            rows_ref[k],
            sums_ref[k],
            total_ref[...],
        )
    state_ref[...] = acc


def output_kernel(
    x_ref, gate_ref, bt_ref, ct_ref, cols_ref, rows_ref, sums_ref, skip_ref, start_ref, gated_ref, squares_ref, state_ref
):
    @pl.when(pl.program_id(0) == 0)
    def _():
        state_ref[...] = start_ref[...]

    for k in range(ROW // Q):
        at = slice(k * Q, (k + 1) * Q)
        gated, squares, state = output_chunk(
            x_ref[at, :],
            gate_ref[at, :],
            bt_ref[:, at],
            ct_ref[:, at],
            cols_ref[k],
            rows_ref[k],
            sums_ref[k],
            skip_ref[...],
            state_ref[...],
        )
        gated_ref[at, :] = gated
        squares_ref[:, at] = squares
        state_ref[...] = state


def norm_kernel(gated_ref, squares_ref, gain_ref, out_ref):
    block = gated_ref.shape[0]
    mean = jnp.sum(squares_ref[...], axis=0, keepdims=True) / D
    scale = lax.rsqrt(mean + EPS)
    gain = gain_ref[...]
    for k in range(block // Q):
        col = jnp.broadcast_to(scale[:, k * Q : (k + 1) * Q], (8, Q)).T[:, 0:1]
        out_ref[k * Q : (k + 1) * Q, :] = (gated_ref[k * Q : (k + 1) * Q, :] * col * gain).astype(BF16)


def per_device(
    features, gate_input, input_map, output_map, step_raw, step_bias, decay_log, skip_gain, norm_gain, tissue
):
    tokens, width = features.shape
    chunks = tokens // Q
    bt = lax.all_gather(input_map.T, "chan", axis=0, tiled=True)
    ct = lax.all_gather(output_map.T, "chan", axis=0, tiled=True)
    bias = jnp.broadcast_to(step_bias[:, None], (H, Q))
    rate = jnp.broadcast_to((-LOG2E * jnp.exp(decay_log))[:, None], (H, Q))
    skip = jnp.repeat(skip_gain, W)[None, :]
    vmem = pl.BlockSpec(memory_space=pltpu.VMEM)
    per_chunk = jax.ShapeDtypeStruct((chunks, 2 * H, Q), F32)
    cols, rows, sums, total = pl.pallas_call(
        functools.partial(decay_kernel, 8),
        out_shape=(per_chunk, per_chunk, per_chunk, jax.ShapeDtypeStruct((H, Q), F32)),
        in_specs=[vmem, vmem, vmem, pl.BlockSpec(memory_space=pltpu.SMEM)],
        out_specs=(vmem, vmem, vmem, vmem),
        name="decays",
    )(step_raw.T, bias, rate, tissue.reshape(-1))
    k = ROW // Q
    token_block = pl.BlockSpec((ROW, width), lambda i: (i, 0))
    map_block = pl.BlockSpec((N, ROW), lambda i: (0, i))
    chunk_block = pl.BlockSpec((k, 2 * H, Q), lambda i: (i, 0, 0))
    whole = lambda shape: pl.BlockSpec(shape, lambda i: (0, 0))
    state = pl.pallas_call(
        state_kernel,
        grid=(tokens // ROW,),
        out_shape=jax.ShapeDtypeStruct((N, width), F32),
        in_specs=[token_block, map_block, chunk_block, chunk_block, whole((H, Q))],
        out_specs=whole((N, width)),
        name="states",
    )(features, bt, rows, sums, total)
    states = lax.all_gather(state, SEQ)
    totals = lax.all_gather(total[:, 0], SEQ)
    bands = lax.axis_size(SEQ)
    me = lax.axis_index(SEQ)
    order = jnp.arange(bands)
    between = (order[None, :] > order[:, None]) & (order[None, :] < me)
    reach = jnp.sum(jnp.where(between[:, :, None], totals[None], 0.0), axis=1)
    factor = jnp.where((order < me)[:, None], jnp.exp2(reach), 0.0)
    start = jnp.sum(jnp.repeat(factor, W, axis=1)[:, None, :] * states, axis=0)
    gated, squares = pl.pallas_call(
        output_kernel,
        grid=(tokens // ROW,),
        out_shape=(jax.ShapeDtypeStruct((tokens, width), F32), jax.ShapeDtypeStruct((1, tokens), F32)),
        in_specs=[
            token_block,
            token_block,
            map_block,
            map_block,
            chunk_block,
            chunk_block,
            chunk_block,
            whole((1, width)),
            whole((N, width)),
        ],
        out_specs=(token_block, pl.BlockSpec((1, ROW), lambda i: (0, i))),
        scratch_shapes=[pltpu.VMEM((N, width), F32)],
        name="outputs",
    )(features, gate_input, bt, ct, cols, rows, sums, skip, start)
    everyone = lax.all_gather(squares[0], "chan")
    return pl.pallas_call(
        norm_kernel,
        grid=(tokens // (2 * ROW),),
        out_shape=jax.ShapeDtypeStruct((tokens, width), BF16),
        in_specs=[
            pl.BlockSpec((2 * ROW, width), lambda i: (i, 0)),
            pl.BlockSpec((4, 2 * ROW), lambda i: (0, i)),
            whole((1, width)),
        ],
        out_specs=pl.BlockSpec((2 * ROW, width), lambda i: (i, 0)),
        name="norm",
    )(gated, everyone, norm_gain[None, :])


def solution(mesh):
    split = Mesh(mesh.devices.reshape(4, 4, 2, mesh.shape["chan"]), (*SEQ, "chan"))
    tokens = P(SEQ, "chan")
    placed = (tokens,) * 5 + (P("chan"),) * 4 + (P(SEQ, None),)
    return jax.shard_map(per_device, mesh=split, in_specs=placed, out_specs=tokens, check_vma=False)
```

time: 505 us -> 225 us (0.45)
  matrix products: 169 us -> 0 us
  local copies, waits for them, and re-layouts: 133 us -> 6.43 us
  other arithmetic: 102 us -> 4.01 us
  Pallas kernels: 0 us -> 71.5 us
  waiting for transfers between devices: 18.4 us -> 49 us
  blocking collectives: 61.4 us -> 79.8 us
    dot_general x73 -> x0, matrix products: 161 us -> none  [the longest x24 84.1 us: row_block(): jnp.einsum('hts,shp->thp', weights, x_row, preferred_element_type=jnp.flo...]
    pallas_call x0 -> x4, Pallas kernels: none -> 71.5 us  [the longest x1 37 us: per_device(): pl.pallas_call(output_kernel, grid=(tokens // ROW,), out_shape=(jax.Shape...]
    unnamed x2 -> x1, blocking collectives: 13.1 us -> 67.5 us
    unnamed x30 -> x11, local copies, waits for them, and re-layouts: 50.2 us -> 2.46 us
    another operation x48 -> x0, other arithmetic: 33.4 us -> none
    all_gather x1 -> x3, waiting for transfers between devices: 18.3 us -> 47.6 us  [the longest x1 35 us: per_device(): bt = lax.all_gather(input_map.T, 'chan', axis=0, tiled=True)]
    transpose x27 -> x0, local copies, waits for them, and re-layouts: 28.1 us -> none
    all_gather x4 -> x1, blocking collectives: 38.5 us -> 12.3 us  [per_device(): everyone = lax.all_gather(squares[0], 'chan')]
  transfers between devices with their start and end apart: 1 -> 3, of which waited for: 1 -> 2; matrix products, arithmetic and copies ran while one was open for 10% -> 4% of each run, Pallas kernels for 0% -> 2%
where the time goes in v1:
time: 225 us
  blocking collectives  79.8 us (35%)
  Pallas kernels  71.5 us (32%)
  waiting for transfers between devices  49 us (22%)
  between operations  13.8 us (6%)
  local copies, waits for them, and re-layouts  6.43 us (3%)
  other arithmetic  4.01 us (2%)
    unnamed x1, blocking collectives  67.5 us
    pallas_call x1, Pallas kernels, per_device(): pl.pallas_call(output_kernel, grid=(tokens // ROW,), out_shape=(jax.Shape...  37 us
    all_gather x1, waiting for transfers between devices, per_device(): bt = lax.all_gather(input_map.T, 'chan', axis=0, tiled=True)  35 us
    pallas_call x1, Pallas kernels, per_device(): pl.pallas_call(state_kernel, grid=(tokens // ROW,), out_shape=jax.ShapeDt...  17.3 us
    pallas_call x1, Pallas kernels, per_device(): pl.pallas_call(norm_kernel, grid=(tokens // (2 * ROW),), out_shape=jax.Sh...  12.7 us
    all_gather x1, waiting for transfers between devices, per_device(): ct = lax.all_gather(output_map.T, 'chan', axis=0, tiled=True)  12.5 us
    all_gather x1, blocking collectives, per_device(): everyone = lax.all_gather(squares[0], 'chan')  12.3 us
    pallas_call x1, Pallas kernels, per_device(): pl.pallas_call(functools.partial(decay_kernel, 8), out_shape=(per_chunk,...  4.56 us
  transfers between devices with their start and end apart: 3, of which 2 were waited for; matrix products, arithmetic and copies ran while one was open for 4% of the time, Pallas kernels for 2%

profile of v1, /device:TPU:0, one launch (start us, length us, event | category | flops | bytes accessed | tf_op | source)
XLA Modules:
  0.0 224.6 jit_solution(4244200518507633586)
XLA Ops:
  6.5 0.0 all-gather.7.cloned.1.call-start
  6.5 0.7 all-gather.7.cloned.1.call-update
  7.3 0.0 all-gather.11.cloned.1.call-start
  7.3 0.8 copy.14
  8.1 0.7 reshape.41.tissue_ref
  8.7 0.7 exponential_multiply_fusion
  9.4 0.7 broadcast_in_dim.60.rate_ref
  10.1 1.3 broadcast_in_dim.59.bias_ref
  11.4 4.6 %decays.1 = (f32[96,8,128]{2,1,0:T(8,128)}, f32[96,8,128]{2,1,0:T(8,128)}, f32[96,8,128]{2,1,0:T(8,128)}, f32[4,128]{1,0:T(4,128)}) custom-call(f32[4,12288]{1,0:T(4,128)} %bitcast.14, f32[4,128]{1,0:T(4,128)} %broadcast_in_dim.59.bias_ref, f32[4,128]{1,0:T(4,128)} %broadcast_in_dim.60.rate_ref, s32[48]{0:T(128)} %reshape.41.tissue_ref), custom_call_target="tpu_custom_call" | custom-call | tf_op jit(solution)/shard_map/decays/pallas_call | solution.py:208
  15.9 35.0 %all-gather.7.cloned.1.call-done.bt_ref = bf16[128,12288]{1,0:T(8,128)(2,1)} async-done(((bf16[32,12288]{1,0:T(8,128)(2,1)}), bf16[128,12288]{1,0:T(8,128)(2,1)}) %all-gather.7.cloned.1.call-update) | async-done | bytes 3145744 | tf_op jit(solution)/shard_map/all_gather | solution.py:201
  51.0 17.3 %states.1 = f32[128,256]{1,0:T(8,128)} custom-call(bf16[12288,256]{1,0:T(8,128)(2,1)} %x_ref.3, bf16[128,12288]{1,0:T(8,128)(2,1)} %all-gather.7.cloned.1.call-done.bt_ref, f32[96,8,128]{2,1,0:T(8,128)} %get-tuple-element.12.rows_ref, f32[96,8,128]{2,1,0:T(8,128)} %get-tuple-element.13.sums_ref, f32[4,128]{1,0:T(4,128)} %get-tuple-element.14.total_ref), custom_call_target="tpu_custom_call" | custom-call | tf_op jit(solution)/shard_map/states/pallas_call | solution.py:220
  68.2 0.0 all-gather.11.cloned.1.call-update
  68.3 0.0 all-gather.9.cloned.1.call-start
  68.3 0.7 all-gather.9.cloned.1.call-update
  69.0 0.1 broadcast_in_dim.61
  69.1 0.7 broadcast_in_dim_reshape.4.skip_ref
  69.7 0.6 dynamic-slice
  71.0 0.1 slice_reduce_fusion
  71.1 0.2 dynamic-update-slice
  71.4 67.5 %all-reduce = f32[128]{0:T(128)S(1)} all-reduce(f32[128]{0:T(128)S(1)} %dynamic-update-slice), channel_id=2, replica_groups=mesh['seq_0'=4,'seq_1'=4,'seq_2'=2,'chan'=4] {'seq_0','seq_1','seq_2'}, use_global_device_ids=true, to_apply=%add | all-reduce | flops 128 | bytes 1024
  138.8 0.1 reshape.42
  138.9 0.1 copy.15
  139.0 0.1 select_reduce_fusion
  139.2 0.1 copy.16
  139.2 0.1 broadcast_in_dim.67
  139.3 0.1 mul.22
  139.5 3.2 %multiply_reduce_fusion.start_ref = f32[128,256]{1,0:T(8,128)} fusion(f32[32,128,256]{2,1,0:T(8,128)} %bitcast.10, f32[32,256]{1,0:T(8,128)S(1)} %mul.22), kind=kLoop, calls=%fused_computation | loop fusion | flops 2064384 | bytes 4358144 | tf_op jit(solution)/shard_map/reduce_sum | solution.py:236
  142.7 12.5 %all-gather.9.cloned.1.call-done.ct_ref = bf16[128,12288]{1,0:T(8,128)(2,1)} async-done(((bf16[32,12288]{1,0:T(8,128)(2,1)}), bf16[128,12288]{1,0:T(8,128)(2,1)}) %all-gather.9.cloned.1.call-update) | async-done | bytes 3145744 | tf_op jit(solution)/shard_map/all_gather | solution.py:202
  155.2 37.0 %outputs.1 = (f32[12288,256]{1,0:T(8,128)}, f32[1,12288]{1,0:T(1,128)}) custom-call(bf16[12288,256]{1,0:T(8,128)(2,1)} %x_ref.3, bf16[12288,256]{1,0:T(8,128)(2,1)} %gate_ref.1, bf16[128,12288]{1,0:T(8,128)(2,1)} %all-gather.7.cloned.1.call-done.bt_ref, bf16[128,12288]{1,0:T(8,128)(2,1)} %all-gather.9.cloned.1.call-done.ct_ref, ...), custom_call_target="tpu_custom_call" | custom-call | tf_op jit(solution)/shard_map/outputs/pallas_call | solution.py:237
  192.2 12.3 %all-gather.2 = f32[4,1,12288]{2,1,0:T(1,128)S(1)} all-gather(f32[1,1,12288]{2,1,0:T(1,128)} %bitcast.15), channel_id=1, replica_groups=mesh['seq_0'=4,'seq_1'=4,'seq_2'=2,'chan'=4] {'chan'}, dimensions={0}, use_global_device_ids=true | all-gather | bytes 245760 | tf_op jit(solution)/shard_map/all_gather | solution.py:256
  204.6 0.8 copy.19
  205.4 12.7 %norm.1 = bf16[12288,256]{1,0:T(8,128)(2,1)} custom-call(f32[12288,256]{1,0:T(8,128)} %get-tuple-element.15.gated_ref, f32[4,12288]{1,0:T(4,128)} %bitcast.11, f32[1,256]{1,0:T(1,128)} %bitcast.16), custom_call_target="tpu_custom_call" | custom-call | tf_op jit(solution)/shard_map/norm/pallas_call | solution.py:257
  (11 shorter events, 0.0 us)
Async XLA Ops:
  6.5 44.4 %all-gather.7.cloned.1.call-start = ((), (), s32[]{:S(2)}) async-start(), calls=%async_computation | async-start | bytes 3932160 | tf_op jit(solution)/shard_map/all_gather | solution.py:201
  7.3 132.2 %all-gather.11.cloned.1.call-start = ((), (), s32[]{:S(2)}) async-start(), calls=%async_computation.2 | async-start | bytes 4325376 | tf_op jit(solution)/shard_map/all_gather | solution.py:228
  51.0 18.0 %copy-start.1 = (f32[4]{0:T(128)S(1)}, f32[4]{0:T(128)}, u32[]{:S(2)}) copy-start(f32[4]{0:T(128)} %param.17) | copy-start | bytes 52
  51.0 18.8 %copy-start.2 = (u32[128]{0:T(128)S(1)}, u32[128]{0:T(128)}, u32[]{:S(2)}) copy-start(u32[128]{0:T(128)} %constant.27) | copy-start | bytes 1540
  51.0 20.0 %copy-start = (f32[4,128]{1,0:T(4,128)S(1)}, f32[4,128]{1,0:T(4,128)}, u32[]{:S(2)}) copy-start(f32[4,128]{1,0:T(4,128)} %get-tuple-element.14.total_ref) | copy-start | bytes 6148
  68.3 87.0 %all-gather.9.cloned.1.call-start = ((), (), s32[]{:S(2)}) async-start(), calls=%async_computation.1 | async-start | bytes 3932160 | tf_op jit(solution)/shard_map/all_gather | solution.py:202
Sparse Core Ops, SparseCore 0:
  9.0 41.9 all-gather.6
  68.4 46.3 all-gather.10
  116.5 38.6 all-gather.8

commit v2 on v1

v2 whole, which is shorter than its diff:
```python
import jax
import jax.numpy as jnp
from jax import lax
from jax.experimental import pallas as pl
from jax.experimental.pallas import tpu as pltpu
from jax.sharding import Mesh
from jax.sharding import PartitionSpec as P

D = 1024
ROW = 512
EPS = 1e-05
SEQ = ("seq_0", "seq_1", "seq_2")
Q = 128
H = 4
W = 64
N = 128
LOG2E = 1.4426950408889634
SEGS = 8
LEAD = 2
BAND = 4
INTRA = 6
FINISH = 6
MESH = pl.DeviceIdType.MESH
F32 = jnp.float32
BF16 = jnp.bfloat16


def softplus(x):
    u = jnp.exp(-jnp.abs(x))
    series = u * (1.0 + u * (-1 / 2 + u * (1 / 3 + u * (-1 / 4 + u * (1 / 5 + u * (-1 / 6 + u * (1 / 7)))))))
    return jnp.maximum(x, 0.0) + jnp.where(u < 0.0625, series, jnp.log(1.0 + u))


def three_parts(a):
    hi = a.astype(BF16)
    rest = a - hi.astype(F32)
    mid = rest.astype(BF16)
    low = (rest - mid.astype(F32)).astype(BF16)
    return hi, mid, low


def exact_dot(a, b):
    hi, mid, low = (jnp.dot(p, b, preferred_element_type=F32) for p in three_parts(a))
    return hi + (mid + low)


def decay_group(g, group, raw_ref, bias, rate, tissue_ref, tri, cols_ref, gaps_ref, rows_ref, sums_ref, total):
    lane = lax.broadcasted_iota(jnp.int32, (H, Q), 1)
    steps = []
    for k in range(group):
        c = g * group + k
        r = c // (ROW // Q)
        raw = raw_ref[:, pl.ds(pl.multiple_of(c * Q, Q), Q)]
        place = lane + (c % (ROW // Q)) * Q
        inside = (place >= tissue_ref[0, r]) & (place < tissue_ref[1, r])
        steps.append(jnp.where(inside, softplus(raw + bias), 0.0))
    step = jnp.concatenate(steps, axis=0)
    log2_decay = step * jnp.concatenate([rate] * group, axis=0)
    both = exact_dot(log2_decay, tri)
    run, tot = both[:, :Q], both[:, Q:]
    key = jnp.minimum(run - jnp.log(step) * LOG2E, 1e30)
    left = jnp.exp2(tot - run) * step
    run_parts, key_parts, grown_parts = (
        [p.astype(F32) for p in three_parts(a)] for a in (run, key, jnp.exp2(run))
    )
    ones = jnp.ones((H, Q), F32)
    row = lax.broadcasted_iota(jnp.int32, (4 * H, Q), 0)
    for k in range(group):
        c = g * group + k
        at = slice(k * H, (k + 1) * H)
        parts = [p[at] for p in run_parts] + [ones] + [p[at] for p in grown_parts] + [jnp.zeros_like(ones)]
        cols_ref[c] = jnp.concatenate(parts, axis=0).astype(BF16)
        for h in range(H):
            block = jnp.where((row < 3 * H) & (row % H == h), 1.0, 0.0)
            for i, p in enumerate(key_parts):
                block = jnp.where(row == 3 * H + i, -p[k * H + h : k * H + h + 1], block)
            gaps_ref[c, :, h * Q : (h + 1) * Q] = block.astype(BF16)
        rows_ref[c] = left[at]
        sums_ref[c] = jnp.concatenate([tot[at], total], axis=0)
        total = total + tot[at]
    return total


def triangle():
    i = lax.broadcasted_iota(jnp.int32, (Q, 2 * Q), 0)
    j = lax.broadcasted_iota(jnp.int32, (Q, 2 * Q), 1)
    return jnp.where((i <= j), 1.0, 0.0).astype(BF16)


def per_head_lanes(rows, k):
    lane = lax.broadcasted_iota(jnp.int32, (1, 2 * W), 1)
    pieces = [
        jnp.where(lane < W, rows[k + 2 * p : k + 2 * p + 1], rows[k + 2 * p + 1 : k + 2 * p + 2])
        for p in range(H // 2)
    ]
    return jnp.concatenate(pieces, axis=1)


def split_pair(x, p):
    lane = lax.broadcasted_iota(jnp.int32, (Q, 2 * W), 1)
    pair = x[:, 2 * W * p : 2 * W * (p + 1)]
    zero = jnp.zeros_like(pair)
    return jnp.concatenate([jnp.where(lane < W, pair, zero), jnp.where(lane < W, zero, pair)], axis=0)


def fresh_state(bt, left, pairs):
    b = bt.astype(F32)
    out = []
    for p in range(H // 2):
        scaled = [(b * left[h : h + 1]).astype(BF16) for h in (2 * p, 2 * p + 1)]
        out.append(jnp.dot(jnp.concatenate(scaled, axis=1), pairs[p], preferred_element_type=F32))
    return jnp.concatenate(out, axis=1)


def row_per_head(values):
    row = lax.broadcasted_iota(jnp.int32, (H, Q), 0)
    out = jnp.full((H, Q), values[0], F32)
    for h in range(1, H):
        out = jnp.where(row == h, values[h], out)
    return out


def join(states, totals, me):
    count = len(states)
    before = before_log = whole = whole_log = 0.0
    reach = jnp.zeros_like(totals[0])
    after = jnp.zeros_like(totals[0])
    for k in reversed(range(count)):
        is_before = k < me
        weight = jnp.where(is_before, jnp.exp2(reach), 0.0)
        before = before + per_head_lanes(weight, 0) * states[k]
        whole = whole + per_head_lanes(jnp.exp2(after), 0) * states[k]
        reach = reach + jnp.where(is_before, totals[k], 0.0)
        after = after + totals[k]
    return (reach, before), (after, whole)


def main_kernel(
    x_hbm,
    gate_hbm,
    b_hbm,
    c_hbm,
    raw_hbm,
    bias_smem,
    decay_smem,
    skip_smem,
    tissue_ref,
    gated_hbm,
    scale_ref,
    raw_ref,
    x_ref,
    gate_ref,
    y_ref,
    silu_ref,
    starts,
    gated_ref,
    maps,
    cols_ref,
    gaps_ref,
    ct_ref,
    rows_ref,
    sums_ref,
    state_ref,
    squares,
    core_s,
    core_l,
    y_s,
    y_l,
    z_s,
    z_l,
    local_sem,
    load_sem,
    gate_sem,
    out_sem,
    map_send,
    map_recv,
    near_send,
    near_recv,
    far_send,
    far_recv,
    sq_send,
    sq_recv,
):
    tokens = x_ref.shape[0]
    chunks = tokens // Q
    per_seg = chunks // SEGS
    seg = tokens // SEGS
    half = maps.shape[3] // 2
    z, yy, core, me = (lax.axis_index(a) for a in (*SEQ, "chan"))
    around = lax.axis_size("chan")
    right, left = lax.rem(me + 1, around), lax.rem(me + around - 1, around)

    def map_load(a, g):
        at = pl.ds(g * seg, seg)
        return pltpu.make_async_copy((b_hbm, c_hbm)[a].at[:, at], maps.at[a, 0, g], load_sem.at[a, g])

    load_x = pltpu.make_async_copy(x_hbm, x_ref, local_sem.at[0])
    load_raw = pltpu.make_async_copy(raw_hbm, raw_ref, local_sem.at[1])

    def gate_load(g):
        at = pl.ds(pl.multiple_of(g * seg, Q), seg)
        return pltpu.make_async_copy(gate_hbm.at[at, :], gate_ref.at[lax.rem(g, 2)], gate_sem.at[g])

    for g in range(SEGS):
        map_load(0, g).start()
    load_raw.start()
    squares[me] = jnp.zeros_like(squares[0])

    barrier = pltpu.get_barrier_semaphore()
    peers = [{"chan": lax.rem(me + d, around)} for d in (1, 2, 3)]
    peers += [{"seq_1": lax.rem(yy + d, 4)} for d in (1, 2, 3)]
    peers += [{"seq_0": lax.rem(z + d, 4)} for d in (1, 2, 3)]
    peers += [{"seq_2": 1 - core}]
    for peer in peers:
        pl.semaphore_signal(barrier, inc=1, device_id=peer, device_id_type=MESH)
    pl.semaphore_wait(barrier, len(peers))

    def remote(src, dst, send, recv, peer):
        return pltpu.make_async_remote_copy(
            src_ref=src, dst_ref=dst, send_sem=send, recv_sem=recv, device_id=peer, device_id_type=MESH
        )

    def map_copy(k, j):
        a, g = j // SEGS, lax.rem(j, SEGS)
        whole, first, second = slice(0, 2 * half), slice(0, half), slice(half, 2 * half)
        plan = (
            (0, 1, whole, right),
            (0, 2, whole, left),
            (1, 3, first, right),
            (2, 3, second, left),
        )
        src, dst, at, peer = plan[k]
        return remote(
            maps.at[a, src, g, at],
            maps.at[a, dst, g, at],
            map_send.at[k, j],
            map_recv.at[k, j],
            {"chan": peer},
        )

    def send_own(j):
        map_copy(0, j).start()
        map_copy(1, j).start()

    def service(j):
        map_copy(0, j).wait_recv()
        map_copy(2, j).start()
        map_copy(1, j).wait_recv()
        map_copy(3, j).start()

        @pl.when(j + LEAD < 2 * SEGS)
        def _():
            send_own(j + LEAD)

    def wait_far(j):
        map_copy(2, j).wait_recv()
        map_copy(3, j).wait_recv()

    for j in range(LEAD):
        map_load(0, j).wait()
        send_own(j)
    for j in range(LEAD, SEGS):
        map_load(0, j).wait()
    for g in range(SEGS):
        map_load(1, g).start()
    load_x.start()
    gate_load(0).start()
    gate_load(1).start()
    load_raw.wait()
    bias = row_per_head([bias_smem[h] for h in range(H)])
    rate = jnp.exp(row_per_head([decay_smem[h] for h in range(H)])) * -LOG2E
    skip = per_head_lanes(row_per_head([skip_smem[h] for h in range(H)]), 0)

    tri = triangle()
    group = 8
    total = lax.fori_loop(
        0,
        chunks // group,
        lambda g, t: decay_group(
            g, group, raw_ref, bias, rate, tissue_ref, tri, cols_ref, gaps_ref, rows_ref, sums_ref, t
        ),
        jnp.zeros((H, Q), F32),
    )
    for g in range(SEGS):
        map_load(1, g).wait()
    load_x.wait()
    state_ref[...] = jnp.zeros_like(state_ref)

    def tokens_of(c):
        return pl.ds(pl.multiple_of(c * Q, Q), Q)

    def map_of(a, c):
        g = c // per_seg
        return maps[a, :, g, :, tokens_of(c - g * per_seg)].reshape(N, Q)

    def band_some(g, i):
        fresh, decay, silu, direct = [], [], [], []
        for k in range(BAND):
            c = g * per_seg + i * BAND + k
            rows = rows_ref[c]
            x = x_ref[tokens_of(c), :]
            pairs = [split_pair(x, p) for p in range(H // 2)]
            fresh.append(fresh_state(map_of(0, c), rows, pairs))
            decay.append(jnp.exp2(per_head_lanes(sums_ref[c], 0)))
            gate = gate_ref[lax.rem(g, 2), tokens_of(i * BAND + k), :].astype(F32) * 0.5
            silu.append(gate + gate * jnp.tanh(gate))
            direct.append(skip * x.astype(F32))
        state = state_ref[...]
        states = []
        for k in range(BAND):
            states.append(state)
            state = decay[k] * state + fresh[k]
        state_ref[...] = state
        for k in range(BAND):
            c = g * per_seg + i * BAND + k
            starts[c] = states[k]
            silu_ref[tokens_of(c), :] = silu[k]
            y_ref[tokens_of(c), :] = direct[k]

    def band_seg(g):
        gate_load(g).wait()
        lax.fori_loop(0, per_seg // BAND, lambda i, carry: (band_some(g, i), carry)[1], 0)

        @pl.when(g + 2 < SEGS)
        def _():
            gate_load(g + 2).start()

    def intra_some(g, i):
        out, turned = [], []
        t = lax.broadcasted_iota(jnp.int32, (Q, Q), 0)
        s = lax.broadcasted_iota(jnp.int32, (Q, Q), 1)
        for k in range(INTRA):
            c = g * per_seg + i * INTRA + k
            x = x_ref[tokens_of(c), :]
            cm = map_of(1, c).T
            turned.append(cm)
            scores = jnp.dot(cm, map_of(0, c), preferred_element_type=F32)
            scores = jnp.where(t >= s, scores, 0.0)
            gap = jnp.dot(cols_ref[c, : 4 * H, :].T, gaps_ref[c], preferred_element_type=F32)
            damp = jnp.exp2(jnp.minimum(gap, 127.0))
            inner = []
            for p in range(H // 2):
                weights = [(scores * damp[:, h * Q : (h + 1) * Q]).astype(BF16) for h in (2 * p, 2 * p + 1)]
                inner.append(
                    jnp.dot(jnp.concatenate(weights, axis=1), split_pair(x, p), preferred_element_type=F32)
                )
            out.append(y_ref[tokens_of(c), :] + jnp.concatenate(inner, axis=1))
        for k in range(INTRA):
            at = tokens_of(g * per_seg + i * INTRA + k)
            y_ref[at, :] = out[k]
            ct_ref[at, :] = turned[k]

    def intra_seg(g):
        lax.fori_loop(0, per_seg // INTRA, lambda i, carry: (intra_some(g, i), carry)[1], 0)

    def finish_some(g, i):
        out, sums_out = [], []
        entering = state_ref[...]
        row = lax.broadcasted_iota(jnp.int32, (4 * H, H * W), 0)
        lane = lax.broadcasted_iota(jnp.int32, (4 * H, H * W), 1)
        spread = jnp.where((row < 3 * H) & (row % H == lane // W), 1.0, 0.0).astype(BF16)
        for k in range(FINISH):
            c = g * per_seg + i * FINISH + k
            at = tokens_of(c)
            state = starts[c] + jnp.exp2(per_head_lanes(sums_ref[c], H)) * entering
            carried = jnp.dot(ct_ref[at, :], state.astype(BF16), preferred_element_type=F32)
            grown = jnp.dot(cols_ref[c, 4 * H :, :].T, spread, preferred_element_type=F32)
            gated = (y_ref[at, :] + grown * carried) * silu_ref[at, :]
            out.append(gated.astype(BF16))
            square = gated * gated
            square = square[:, :Q] + square[:, Q:]
            sums_out.append(jnp.sum(square.T, axis=0, keepdims=True))
        for k in range(FINISH):
            gated_ref[lax.rem(g, 2), tokens_of(i * FINISH + k), :] = out[k]
            squares[me, g, pl.ds(i * FINISH + k, 1), :] = sums_out[k]

    def gated_copy(g):
        at = pl.ds(pl.multiple_of(g * seg, Q), seg)
        return pltpu.make_async_copy(gated_ref.at[lax.rem(g, 2)], gated_hbm.at[at, :], out_sem.at[g])

    def square_copies(g):
        return [
            remote(
                squares.at[me, g],
                squares.at[me, g],
                sq_send.at[d - 1, g],
                sq_recv.at[d - 1, g],
                {"chan": lax.rem(me + d, around)},
            )
            for d in (1, 2, 3)
        ]

    def finish_seg(g):
        @pl.when(g >= 2)
        def _():
            gated_copy(g - 2).wait()

        lax.fori_loop(0, per_seg // FINISH, lambda i, carry: (finish_some(g, i), carry)[1], 0)
        gated_copy(g).start()
        for copy in square_copies(g):
            copy.start()

    def exchange(slots_s, slots_l, sends, recvs, axis, at):
        size = slots_s.shape[0]
        copies = []
        for d in range(1, size):
            peer = {axis: lax.rem(at + d, size)}
            copies.append(remote(slots_s.at[at], slots_s.at[at], sends(d, 0), recvs(d, 0), peer))
            copies.append(remote(slots_l.at[at], slots_l.at[at], sends(d, 1), recvs(d, 1), peer))
        return copies

    def put(slots_s, slots_l, at, pair):
        slots_l[at] = pair[0]
        slots_s[at] = pair[1].astype(slots_s.dtype)

    def get(slots_s, slots_l, at):
        size = slots_s.shape[0]
        return join([slots_s[k].astype(F32) for k in range(size)], [slots_l[k] for k in range(size)], at)

    service(0)

    def band_step(j, carry):
        service(j)
        wait_far(j - 1)
        band_seg(j - 1)
        return carry

    lax.fori_loop(1, SEGS + 1, band_step, 0)

    near = exchange(core_s, core_l, lambda d, k: near_send.at[k], lambda d, k: near_recv.at[k], "seq_2", core)
    along_y = exchange(
        y_s, y_l, lambda d, k: far_send.at[0, d - 1, k], lambda d, k: far_recv.at[0, d - 1, k], "seq_1", yy
    )
    along_z = exchange(
        z_s, z_l, lambda d, k: far_send.at[1, d - 1, k], lambda d, k: far_recv.at[1, d - 1, k], "seq_0", z
    )

    def inner_step(g, carry=0):
        service(SEGS + g + 1)
        wait_far(SEGS + g)
        intra_seg(g)
        return carry

    def finish_step(g, carry=0):
        finish_seg(g)
        return carry

    put(core_s, core_l, core, (total, state_ref[...]))
    for copy in near:
        copy.start()
    inner_step(0)
    for copy in near:
        copy.wait()
    in_core, chip = get(core_s, core_l, core)
    put(y_s, y_l, yy, chip)
    for copy in along_y:
        copy.start()
    lax.fori_loop(1, 3, inner_step, 0)
    for copy in along_y:
        copy.wait()
    in_y, plane = get(y_s, y_l, yy)
    put(z_s, z_l, z, plane)
    for copy in along_z:
        copy.start()
    lax.fori_loop(3, 5, inner_step, 0)
    for copy in along_z:
        copy.wait()
    in_z, _ = get(z_s, z_l, z)
    lanes = lambda log: per_head_lanes(jnp.exp2(log), 0)
    state_ref[...] = lanes(in_core[0]) * (lanes(in_y[0]) * in_z[1] + in_y[1]) + in_core[1]

    finish_seg(0)
    inner_step(5)
    lax.fori_loop(1, 3, finish_step, 0)
    inner_step(6)
    lax.fori_loop(3, 7, finish_step, 0)
    wait_far(2 * SEGS - 1)
    intra_seg(SEGS - 1)
    finish_seg(SEGS - 1)

    def close(g, carry):
        for copy in square_copies(g):
            copy.wait()
        mean = (squares[0, g] + squares[1, g] + squares[2, g] + squares[3, g]) / D
        scale_ref[g] = lax.rsqrt(mean + EPS)
        return carry

    lax.fori_loop(0, SEGS, close, 0)
    gated_copy(SEGS - 2).wait()
    gated_copy(SEGS - 1).wait()

    def drain(j, carry):
        for k in range(4):
            map_copy(k, j).wait_send()
        return carry

    lax.fori_loop(0, 2 * SEGS, drain, 0)


def norm_kernel(gated_hbm, scale_ref, gain_ref, out_hbm, gated_ref, out_ref, load_sem, store_sem):
    seg = gated_ref.shape[0] // SEGS

    def load(g):
        at = pl.ds(g * seg, seg)
        return pltpu.make_async_copy(gated_hbm.at[at, :], gated_ref.at[at, :], load_sem.at[g])

    def store(g):
        at = pl.ds(g * seg, seg)
        return pltpu.make_async_copy(out_ref.at[at, :], out_hbm.at[at, :], store_sem.at[g])

    for g in range(SEGS):
        load(g).start()

    def one(g, carry):
        col = scale_ref[g].T
        load(g).wait()
        for k in range(seg // Q):
            at = pl.ds(pl.multiple_of(g * seg + k * Q, Q), Q)
            out_ref[at, :] = (gated_ref[at, :].astype(F32) * col[:, k : k + 1] * gain_ref[...]).astype(BF16)
        store(g).start()
        return carry

    lax.fori_loop(0, SEGS, one, 0)
    for g in range(SEGS):
        store(g).wait()


def per_device(
    features, gate_input, input_map, output_map, step_raw, step_bias, decay_log, skip_gain, norm_gain, tissue
):
    tokens, width = features.shape
    chunks = tokens // Q
    vmem = pl.BlockSpec(memory_space=pltpu.VMEM)
    hbm = pl.BlockSpec(memory_space=pl.ANY)
    around = lax.axis_size("chan")
    dma = pltpu.SemaphoreType.DMA
    slots = lambda n, dtype: [pltpu.VMEM((n, N, width), dtype), pltpu.VMEM((n, H, Q), F32)]
    gated, scale = pl.pallas_call(
        main_kernel,
        out_shape=(
            jax.ShapeDtypeStruct((tokens, width), BF16),
            jax.ShapeDtypeStruct((SEGS, 16, Q), F32),
        ),
        in_specs=[hbm] * 5 + [pl.BlockSpec(memory_space=pltpu.SMEM)] * 4,
        out_specs=(hbm, vmem),
        scratch_shapes=[
            pltpu.VMEM((H, tokens), F32),
            pltpu.VMEM((tokens, width), BF16),
            pltpu.VMEM((2, tokens // SEGS, width), BF16),
            pltpu.VMEM((tokens, width), F32),
            pltpu.VMEM((tokens, width), F32),
            pltpu.VMEM((chunks, N, width), F32),
            pltpu.VMEM((2, tokens // SEGS, width), BF16),
            pltpu.VMEM((2, around, SEGS, N // around, tokens // SEGS), BF16),
            pltpu.VMEM((chunks, 8 * H, Q), BF16),
            pltpu.VMEM((chunks, 4 * H, H * Q), BF16),
            pltpu.VMEM((tokens, N), BF16),
            pltpu.VMEM((chunks, H, Q), F32),
            pltpu.VMEM((chunks, 2 * H, Q), F32),
            pltpu.VMEM((N, width), F32),
            pltpu.VMEM((around, SEGS, 16, Q), F32),
            *slots(2, F32),
            *slots(4, BF16),
            *slots(4, BF16),
            dma((2,)),
            dma((2, SEGS)),
            dma((SEGS,)),
            dma((SEGS,)),
            dma((4, 2 * SEGS)),
            dma((4, 2 * SEGS)),
            dma((2,)),
            dma((2,)),
            dma((2, 3, 2)),
            dma((2, 3, 2)),
            dma((3, SEGS)),
            dma((3, SEGS)),
        ],
        compiler_params=pltpu.CompilerParams(
            collective_id=0, has_side_effects=True, vmem_limit_bytes=67043328
        ),
        name="scan",
    )(features, gate_input, input_map.T, output_map.T, step_raw.T, step_bias, decay_log, skip_gain, tissue.T)
    return pl.pallas_call(
        norm_kernel,
        out_shape=jax.ShapeDtypeStruct((tokens, width), BF16),
        in_specs=[hbm, vmem, vmem],
        out_specs=hbm,
        scratch_shapes=[
            pltpu.VMEM((tokens, width), BF16),
            pltpu.VMEM((tokens, width), BF16),
            dma((SEGS,)),
            dma((SEGS,)),
        ],
        compiler_params=pltpu.CompilerParams(vmem_limit_bytes=63 * 1024 * 1024),
        name="norm",
    )(gated, scale, norm_gain[None, :])


def solution(mesh):
    split = Mesh(mesh.devices.reshape(4, 4, 2, mesh.shape["chan"]), (*SEQ, "chan"))
    tokens = P(SEQ, "chan")
    placed = (tokens,) * 5 + (P("chan"),) * 4 + (P(SEQ, None),)
    return jax.shard_map(per_device, mesh=split, in_specs=placed, out_specs=tokens, check_vma=False)
```

time: 225 us -> 84.7 us (0.38)
  blocking collectives: 79.8 us -> 0 us
  waiting for transfers between devices: 49 us -> 0 us
  between operations: 13.8 us -> 0.01 us
  Pallas kernels: 71.5 us -> 84.5 us
  local copies, waits for them, and re-layouts: 6.43 us -> 0 us
  other arithmetic: 4.01 us -> 0 us
    unnamed x1 -> x0, blocking collectives: 67.5 us -> none
    all_gather x3 -> x0, waiting for transfers between devices: 47.6 us -> none  [the longest x1 35 us: per_device(): bt = lax.all_gather(input_map.T, 'chan', axis=0, tiled=True)]
    pallas_call x4 -> x2, Pallas kernels: 71.5 us -> 84.5 us  [the longest x1 78.4 us: per_device(): pl.pallas_call(main_kernel, out_shape=(jax.ShapeDtypeStruct((tokens, widt...]
    all_gather x1 -> x0, blocking collectives: 12.3 us -> none  [per_device(): everyone = lax.all_gather(squares[0], 'chan')]
    reduce_sum x2 -> x0, other arithmetic: 3.32 us -> none  [the longest x1 3.23 us: per_device(): start = jnp.sum(jnp.repeat(factor, W, axis=1)[:, None, :] * states, axis=0)]
    unnamed x11 -> x0, local copies, waits for them, and re-layouts: 2.46 us -> none
  transfers between devices with their start and end apart: 3 -> 0, of which waited for: 2 -> 0; matrix products, arithmetic and copies ran while one was open for 4% -> 0% of each run, Pallas kernels for 2% -> 0%
where the time goes in v2:
time: 84.7 us; the launch traced here: 84.5 us
  Pallas kernels  84.5 us (100%)
    pallas_call x1, Pallas kernels, per_device(): pl.pallas_call(main_kernel, out_shape=(jax.ShapeDtypeStruct((tokens, widt...  78.4 us
    pallas_call x1, Pallas kernels, per_device(): pl.pallas_call(norm_kernel, out_shape=jax.ShapeDtypeStruct((tokens, width...  6.12 us

profile of v2, /device:TPU:0, one launch (start us, length us, event | category | flops | bytes accessed | tf_op | source)
XLA Modules:
  0.0 84.5 jit_solution(16890656659170515956)
XLA Ops:
  0.0 78.4 %scan.1 = (bf16[12288,256]{1,0:T(8,128)(2,1)}, f32[8,16,128]{2,1,0:T(8,128)}) custom-call(bf16[12288,256]{1,0:T(8,128)(2,1)} %x_hbm.1, bf16[12288,256]{1,0:T(8,128)(2,1)} %gate_hbm.1, bf16[32,12288]{1,0:T(8,128)(2,1)} %bitcast.5, bf16[32,12288]{1,0:T(8,128)(2,1)} %bitcast.6, f32[4,12288]{1,0:T(4,128)} %bitcast.7, f32[4]{0:T(128)} %bias_smem.1, f32[4]{0:T(128)} %decay_smem.1, ...), custom_call_target="tpu_custom_call" | custom-call | tf_op jit(solution)/shard_map/scan/pallas_call | solution.py:538
  78.4 6.1 %norm.1 = bf16[12288,256]{1,0:T(8,128)(2,1)} custom-call(bf16[12288,256]{1,0:T(8,128)(2,1)} %get-tuple-element.7.gated_hbm, f32[8,16,128]{2,1,0:T(8,128)} %get-tuple-element.8.scale_ref, f32[1,256]{1,0:T(1,128)} %bitcast.9), custom_call_target="tpu_custom_call" | custom-call | tf_op jit(solution)/shard_map/norm/pallas_call | solution.py:583

commit v3 on v2

--- a/solution.py
+++ b/solution.py
@@ -185,10 +185,8 @@
     chunks = tokens // Q
     per_seg = chunks // SEGS
     seg = tokens // SEGS
-    half = maps.shape[3] // 2
     z, yy, core, me = (lax.axis_index(a) for a in (*SEQ, "chan"))
     around = lax.axis_size("chan")
-    right, left = lax.rem(me + 1, around), lax.rem(me + around - 1, around)
 
     def map_load(a, g):
         at = pl.ds(g * seg, seg)
@@ -220,41 +218,34 @@
             src_ref=src, dst_ref=dst, send_sem=send, recv_sem=recv, device_id=peer, device_id_type=MESH
         )
 
-    def map_copy(k, j):
+    def own_copy(side, j):
         a, g = j // SEGS, lax.rem(j, SEGS)
-        whole, first, second = slice(0, 2 * half), slice(0, half), slice(half, 2 * half)
-        plan = (
-            (0, 1, whole, right),
-            (0, 2, whole, left),
-            (1, 3, first, right),
-            (2, 3, second, left),
+        peer = {"chan": lax.rem(me + 1 + 2 * side, around)}
+        return remote(
+            maps.at[a, 0, g], maps.at[a, 1 + side, g], map_send.at[side, j], map_recv.at[side, j], peer
         )
-        src, dst, at, peer = plan[k]
-        return remote(
-            maps.at[a, src, g, at],
-            maps.at[a, dst, g, at],
-            map_send.at[k, j],
-            map_recv.at[k, j],
-            {"chan": peer},
-        )
+
+    def far_copy(j):
+        a, g, side = j // SEGS, lax.rem(j, SEGS), lax.rem(j, 2)
+        peer = {"chan": lax.rem(me + 1 + 2 * side, around)}
+        return remote(maps.at[a, 1 + side, g], maps.at[a, 3, g], map_send.at[2, j], map_recv.at[2, j], peer)
 
     def send_own(j):
-        map_copy(0, j).start()
-        map_copy(1, j).start()
+        own_copy(0, j).start()
+        own_copy(1, j).start()
 
     def service(j):
-        map_copy(0, j).wait_recv()
-        map_copy(2, j).start()
-        map_copy(1, j).wait_recv()
-        map_copy(3, j).start()
+        side = lax.rem(j, 2)
+        own_copy(side, j).wait_recv()
+        far_copy(j).start()
+        own_copy(1 - side, j).wait_recv()
 
         @pl.when(j + LEAD < 2 * SEGS)
         def _():
             send_own(j + LEAD)
 
     def wait_far(j):
-        map_copy(2, j).wait_recv()
-        map_copy(3, j).wait_recv()
+        far_copy(j).wait_recv()
 
     for j in range(LEAD):
         map_load(0, j).wait()
@@ -326,29 +317,32 @@
             gate_load(g + 2).start()
 
     def intra_some(g, i):
-        out, turned = [], []
         t = lax.broadcasted_iota(jnp.int32, (Q, Q), 0)
         s = lax.broadcasted_iota(jnp.int32, (Q, Q), 1)
+        def ahead(k):
+            c = g * per_seg + i * INTRA + k
+            cm = map_of(1, c).T
+            gap = jnp.dot(cols_ref[c, : 4 * H, :].T, gaps_ref[c], preferred_element_type=F32)
+            scores = jnp.dot(cm, map_of(0, c), preferred_element_type=F32)
+            return cm, scores, gap
+
+        coming = [ahead(0), ahead(1)]
         for k in range(INTRA):
             c = g * per_seg + i * INTRA + k
+            if k + 2 < INTRA:
+                coming.append(ahead(k + 2))
+            cm, scores, gap = coming[k]
+            ct_ref[tokens_of(c), :] = cm
             x = x_ref[tokens_of(c), :]
-            cm = map_of(1, c).T
-            turned.append(cm)
-            scores = jnp.dot(cm, map_of(0, c), preferred_element_type=F32)
             scores = jnp.where(t >= s, scores, 0.0)
-            gap = jnp.dot(cols_ref[c, : 4 * H, :].T, gaps_ref[c], preferred_element_type=F32)
-            damp = jnp.exp2(jnp.minimum(gap, 127.0))
             inner = []
             for p in range(H // 2):
-                weights = [(scores * damp[:, h * Q : (h + 1) * Q]).astype(BF16) for h in (2 * p, 2 * p + 1)]
+                damp = jnp.exp2(jnp.minimum(gap[:, 2 * p * Q : 2 * (p + 1) * Q], 127.0))
+                weights = [(scores * damp[:, h * Q : (h + 1) * Q]).astype(BF16) for h in range(2)]
                 inner.append(
                     jnp.dot(jnp.concatenate(weights, axis=1), split_pair(x, p), preferred_element_type=F32)
                 )
-            out.append(y_ref[tokens_of(c), :] + jnp.concatenate(inner, axis=1))
-        for k in range(INTRA):
-            at = tokens_of(g * per_seg + i * INTRA + k)
-            y_ref[at, :] = out[k]
-            ct_ref[at, :] = turned[k]
+            y_ref[tokens_of(c), :] += jnp.concatenate(inner, axis=1)
 
     def intra_seg(g):
         lax.fori_loop(0, per_seg // INTRA, lambda i, carry: (intra_some(g, i), carry)[1], 0)
@@ -490,8 +484,9 @@
     gated_copy(SEGS - 1).wait()
 
     def drain(j, carry):
-        for k in range(4):
-            map_copy(k, j).wait_send()
+        own_copy(0, j).wait_send()
+        own_copy(1, j).wait_send()
+        far_copy(j).wait_send()
         return carry
 
     lax.fori_loop(0, 2 * SEGS, drain, 0)
@@ -566,8 +561,8 @@
             dma((2, SEGS)),
             dma((SEGS,)),
             dma((SEGS,)),
-            dma((4, 2 * SEGS)),
-            dma((4, 2 * SEGS)),
+            dma((3, 2 * SEGS)),
+            dma((3, 2 * SEGS)),
             dma((2,)),
             dma((2,)),
             dma((2, 3, 2)),

time: 84.7 us -> 80.6 us (0.952)
  Pallas kernels: 84.5 us -> 80.4 us
    pallas_call x1, Pallas kernels: 78.4 us -> 74.3 us  [per_device(): pl.pallas_call(main_kernel, out_shape=(jax.ShapeDtypeStruct((tokens, widt...]
where the time goes in v3:
time: 80.6 us; the launch traced here: 80.5 us
  Pallas kernels  80.4 us (100%)
    pallas_call x1, Pallas kernels, per_device(): pl.pallas_call(main_kernel, out_shape=(jax.ShapeDtypeStruct((tokens, widt...  74.3 us
    pallas_call x1, Pallas kernels, per_device(): pl.pallas_call(norm_kernel, out_shape=jax.ShapeDtypeStruct((tokens, width...  6.12 us

profile of v3, /device:TPU:0, one launch (start us, length us, event | category | flops | bytes accessed | tf_op | source)
XLA Modules:
  0.0 80.5 jit_solution(10342207076602664676)
XLA Ops:
  0.0 74.3 %scan.1 = (bf16[12288,256]{1,0:T(8,128)(2,1)}, f32[8,16,128]{2,1,0:T(8,128)}) custom-call(bf16[12288,256]{1,0:T(8,128)(2,1)} %x_hbm.1, bf16[12288,256]{1,0:T(8,128)(2,1)} %gate_hbm.1, bf16[32,12288]{1,0:T(8,128)(2,1)} %bitcast.5, bf16[32,12288]{1,0:T(8,128)(2,1)} %bitcast.6, f32[4,12288]{1,0:T(4,128)} %bitcast.7, f32[4]{0:T(128)} %bias_smem.1, f32[4]{0:T(128)} %decay_smem.1, ...), custom_call_target="tpu_custom_call" | custom-call | tf_op jit(solution)/shard_map/scan/pallas_call | solution.py:533
  74.3 6.1 %norm.1 = bf16[12288,256]{1,0:T(8,128)(2,1)} custom-call(bf16[12288,256]{1,0:T(8,128)(2,1)} %get-tuple-element.7.gated_hbm, f32[8,16,128]{2,1,0:T(8,128)} %get-tuple-element.8.scale_ref, f32[1,256]{1,0:T(1,128)} %bitcast.9), custom_call_target="tpu_custom_call" | custom-call | tf_op jit(solution)/shard_map/norm/pallas_call | solution.py:578

commit v4 on v3

--- a/solution.py
+++ b/solution.py
@@ -18,8 +18,8 @@
 SEGS = 8
 LEAD = 2
 BAND = 4
-INTRA = 6
-FINISH = 6
+INTRA = 12
+FINISH = 12
 MESH = pl.DeviceIdType.MESH
 F32 = jnp.float32
 BF16 = jnp.bfloat16
@@ -225,27 +225,31 @@
             maps.at[a, 0, g], maps.at[a, 1 + side, g], map_send.at[side, j], map_recv.at[side, j], peer
         )
 
-    def far_copy(j):
-        a, g, side = j // SEGS, lax.rem(j, SEGS), lax.rem(j, 2)
+    def far_copy(side, j):
+        a, g = j // SEGS, lax.rem(j, SEGS)
+        half = maps.shape[3] // 2
+        at = slice(side * half, (side + 1) * half)
         peer = {"chan": lax.rem(me + 1 + 2 * side, around)}
-        return remote(maps.at[a, 1 + side, g], maps.at[a, 3, g], map_send.at[2, j], map_recv.at[2, j], peer)
+        return remote(
+            maps.at[a, 1 + side, g, at], maps.at[a, 3, g, at], map_send.at[2 + side, j], map_recv.at[2 + side, j], peer
+        )
 
     def send_own(j):
         own_copy(0, j).start()
         own_copy(1, j).start()
 
     def service(j):
-        side = lax.rem(j, 2)
-        own_copy(side, j).wait_recv()
-        far_copy(j).start()
-        own_copy(1 - side, j).wait_recv()
+        for side in range(2):
+            own_copy(side, j).wait_recv()
+            far_copy(side, j).start()
 
         @pl.when(j + LEAD < 2 * SEGS)
         def _():
             send_own(j + LEAD)
 
     def wait_far(j):
-        far_copy(j).wait_recv()
+        far_copy(0, j).wait_recv()
+        far_copy(1, j).wait_recv()
 
     for j in range(LEAD):
         map_load(0, j).wait()
@@ -486,7 +490,8 @@
     def drain(j, carry):
         own_copy(0, j).wait_send()
         own_copy(1, j).wait_send()
-        far_copy(j).wait_send()
+        far_copy(0, j).wait_send()
+        far_copy(1, j).wait_send()
         return carry
 
     lax.fori_loop(0, 2 * SEGS, drain, 0)
@@ -561,8 +566,8 @@
             dma((2, SEGS)),
             dma((SEGS,)),
             dma((SEGS,)),
-            dma((3, 2 * SEGS)),
-            dma((3, 2 * SEGS)),
+            dma((4, 2 * SEGS)),
+            dma((4, 2 * SEGS)),
             dma((2,)),
             dma((2,)),
             dma((2, 3, 2)),

time: 80.6 us -> 77.7 us (0.964)
  Pallas kernels: 80.4 us -> 77.6 us
    pallas_call x1, Pallas kernels: 74.3 us -> 71.4 us  [per_device(): pl.pallas_call(main_kernel, out_shape=(jax.ShapeDtypeStruct((tokens, widt...]
where the time goes in v4:
time: 77.7 us; the launch traced here: 77.6 us
  Pallas kernels  77.6 us (100%)
    pallas_call x1, Pallas kernels, per_device(): pl.pallas_call(main_kernel, out_shape=(jax.ShapeDtypeStruct((tokens, widt...  71.4 us
    pallas_call x1, Pallas kernels, per_device(): pl.pallas_call(norm_kernel, out_shape=jax.ShapeDtypeStruct((tokens, width...  6.12 us

profile of v4, /device:TPU:0, one launch (start us, length us, event | category | flops | bytes accessed | tf_op | source)
XLA Modules:
  0.0 77.6 jit_solution(13218096775851966280)
XLA Ops:
  0.0 71.4 %scan.1 = (bf16[12288,256]{1,0:T(8,128)(2,1)}, f32[8,16,128]{2,1,0:T(8,128)}) custom-call(bf16[12288,256]{1,0:T(8,128)(2,1)} %x_hbm.1, bf16[12288,256]{1,0:T(8,128)(2,1)} %gate_hbm.1, bf16[32,12288]{1,0:T(8,128)(2,1)} %bitcast.5, bf16[32,12288]{1,0:T(8,128)(2,1)} %bitcast.6, f32[4,12288]{1,0:T(4,128)} %bitcast.7, f32[4]{0:T(128)} %bias_smem.1, f32[4]{0:T(128)} %decay_smem.1, ...), custom_call_target="tpu_custom_call" | custom-call | tf_op jit(solution)/shard_map/scan/pallas_call | solution.py:538
  71.4 6.1 %norm.1 = bf16[12288,256]{1,0:T(8,128)(2,1)} custom-call(bf16[12288,256]{1,0:T(8,128)(2,1)} %get-tuple-element.7.gated_hbm, f32[8,16,128]{2,1,0:T(8,128)} %get-tuple-element.8.scale_ref, f32[1,256]{1,0:T(1,128)} %bitcast.9), custom_call_target="tpu_custom_call" | custom-call | tf_op jit(solution)/shard_map/norm/pallas_call | solution.py:583
